TPU v7x, 256 devices: a whole 4x4x8 slice. The times are simulated.
256 devices in a mesh: tm: 8 (over x, y_lo), space: 32 (over z, y_hi, core).
Axes of the slice: x: 4, y: 4 (y_hi: 2, y_lo: 2; y = y_hi * 2 + y_lo), z: 8, core: 2. Of those that a mesh axis runs over, the one named last changes fastest.
Arguments:
- source: float32 [16, 4096, 5, 128], P('tm', 'space'), may hold values from -6 to 6
- terminal: float32 [4096, 5, 128], P('space'), may hold values from -6 to 6
- jacobian: float32 [8, 4096, 5, 5, 128], P('tm', 'space')
- face_coef: float32 [4096, 6, 128], P('space'), may hold values from 0.1 to 0.5
- cell_coef: float32 [4096, 128], P('space'), may hold values from 0.1 to 0.5
- neighbours: int32 [4096, 6], P('space'), may hold values from 0 to 160, as said below
- send_blocks: int32 [32, 2, 16], P('space'), may hold values from 0 to 127, as said below
- live_count: int32 [32], P('space'), may hold values from 64 to 128, as said below
- volume: float32 [4096, 128], P('space'), may hold values from 0.5 to 2
- shape_field: float32 [4096, 5, 128], P('space'), may hold values from -6 to 6
- weights: float32 [16], P('tm'), may hold values from 0.25 to 4
Outputs:
- adjoint: float32 [16, 4096, 5, 128], P('tm', 'space')
- sensitivity: float32 [4096], P('space')
Inputs may be any that keep to these rules, and one draw needn't show every extreme that they name: `live_count`: some device has 128 live blocks in every draw. `send_blocks`: each index names a live block of its own device. `neighbours`: a slot below 128 names a live block of the same device; 128 to 159 name received blocks, those of the lower device first; 160 is an empty slot.
All inputs are finite; a program needn't handle non-finite values.
Results may differ from a plain program's by a relative error of at most 0.00016.
Values sent between devices are 32-bit elements; how exact they have to be, the bound alone decides.
A program may use at most 64 MiB of HBM per device.

v0:
```python
import jax
import jax.numpy as jnp
from jax import lax
from jax.sharding import PartitionSpec as P

ITERS = 3


inverse_step = 6.0


def from_behind(value, axis, steps):
    count = lax.axis_size(axis)
    first, last = (max(0, -steps), min(count, count - steps))
    return lax.ppermute(value, axis, [(source, source + steps) for source in range(first, last)])


def copy_for_each(x, axis):
    copies = jnp.broadcast_to(x, (lax.axis_size(axis), *x.shape))
    return lax.all_to_all(copies, axis, split_axis=0, concat_axis=0, tiled=True)


def taken_together(x, axis):
    return copy_for_each(x, axis).sum(axis=0)


def pad_local(field):
    return jnp.pad(field, ((0, 0), (0, 0), (1, 1)))


def make_operator(face_coef, cell_coef, neighbours, mass, to_lower, to_higher, sides):
    highest = lax.Precision.HIGHEST
    along_coef = cell_coef[:, None, :]

    def operate(field, jac):
        from_lower = from_behind(field[to_higher], "space", 1)
        from_higher = from_behind(field[to_lower], "space", -1)
        blank = jnp.zeros((1,) + field.shape[1:], jnp.float32)
        extended = jnp.concatenate([field, from_lower, from_higher, blank], axis=0)
        gathered = extended[neighbours]
        coupled = jnp.einsum("bnc,bnkc->bkc", face_coef, gathered, precision=highest)
        own = jnp.einsum("bijc,bic->bjc", jac, field, precision=highest)
        widened = sides(field)
        beside = widened[:, :, :-2] + widened[:, :, 2:]
        return mass * field + own - coupled - along_coef * beside

    return operate


def make_precond(jac, mass, face_coef, cell_coef):
    diagonal = jnp.stack([jac[:, k, k, :] for k in range(jac.shape[1])], axis=1)
    return 1.0 / (
        mass + diagonal + jnp.sum(face_coef, axis=1)[:, None, :] + 2.0 * cell_coef[:, None, :]
    )


def sweep_levels(incoming, sources, jac, precond, mass, live, operate):

    def level_step(later, level_source):
        rhs = level_source + mass * later
        field = later
        for sweep in range(ITERS):
            field = live * (field + precond * (rhs - operate(field, jac)))
        return (field, field)

    return lax.scan(level_step, incoming, sources, reverse=True)


def per_device(
    source,
    terminal,
    jacobian,
    face_coef,
    cell_coef,
    neighbours,
    send_blocks,
    live_count,
    volume,
    shape_field,
    weights,
):
    nblocks = terminal.shape[0]
    live = (lax.iota(jnp.int32, nblocks) < live_count[0]).astype(jnp.float32)[:, None, None]
    mass = (inverse_step * volume)[:, None, :]
    to_lower = send_blocks[0, 0]
    to_higher = send_blocks[0, 1]
    rounds = lax.axis_size("tm")
    jac = jacobian[0]
    precond = make_precond(jac, mass, face_coef, cell_coef)
    operate = make_operator(face_coef, cell_coef, neighbours, mass, to_lower, to_higher, pad_local)

    def slab(incoming):
        return sweep_levels(incoming, source, jac, precond, mass, live, operate)

    is_last = lax.axis_index("tm") == rounds - 1
    start = live * terminal

    def turn(step_index, incoming):
        first, fields = slab(incoming)
        moved = from_behind(first, "tm", -1)
        return jnp.where(is_last, start, moved)

    incoming = lax.fori_loop(0, rounds - 1, turn, start)
    first, fields = slab(incoming)
    sensitivity = taken_together(
        jnp.sum(weights[:, None] * jnp.sum(fields * shape_field[None], axis=(2, 3)), axis=0), "tm"
    )
    return (fields, sensitivity)


def solution(mesh):
    return jax.shard_map(
        per_device,
        mesh=mesh,
        in_specs=(
            P("tm", "space", None, None),
            P("space", None, None),
            P("tm", "space", None, None, None),
            P("space", None, None),
            P("space", None),
            P("space", None),
            P("space", None, None),
            P("space"),
            P("space", None),
            P("space", None, None),
            P("tm"),
        ),
        out_specs=(P("tm", "space", None, None), P("space")),
        check_vma=False,
    )
```

profile of v0, /device:TPU:96, one launch (start us, length us, event | category | flops | bytes accessed | tf_op | source)
XLA Modules:
  0.0 1295.7 jit_solution(17971713993202420043)
XLA Ops:
  16.2 1106.3 %while.60 = (s32[]{:T(128)}, f32[128,5,128]{2,1,0:T(8,128)S(1)}, pred[]{:T(512)}, f32[2,128,5,128]{3,2,1,0:T(8,128)}, f32[128,1,128]{2,0,1:T(8,128)S(1)}, /*inde...) while((s32[]{:T(128)}, f32[128,5,128]{2,1,0:T(8,128)S(1)}, ...), condition=%wide.region_4.5_spmd.clone, body=%wide.region_1.4_spmd.clone.sunk | while | flops 8797413 | bytes 66983056 | solution.py:103
  17.5 135.0 %while.62 = (s32[]{:T(128)}, f32[128,5,128]{2,1,0:T(8,128)S(1)}, f32[128,1,1]{0,2,1:T(1,128)}, f32[2,128,5,128]{3,2,1,0:T(8,128)}, f32[128,1,128]{2,0,1:T(8,128)...) while((s32[]{:T(128)}, f32[128,5,128]{2,1,0:T(8,128)S(1)}, ...), condition=%wide.region_3.3_spmd, body=%wide.region_2.2_spmd.sunk | while | flops 8715235 | bytes 64688432 | solution.py:66
  153.8 9.9 collective-permute-done.12
  166.0 145.4 %while.62 = (s32[]{:T(128)}, f32[128,5,128]{2,1,0:T(8,128)S(1)}, f32[128,1,1]{0,2,1:T(1,128)}, f32[2,128,5,128]{3,2,1,0:T(8,128)}, f32[128,1,128]{2,0,1:T(8,128)...) while((s32[]{:T(128)}, f32[128,5,128]{2,1,0:T(8,128)S(1)}, ...), condition=%wide.region_3.3_spmd, body=%wide.region_2.2_spmd.sunk | while | flops 8715235 | bytes 64688432 | solution.py:66
  217.4 8.6 collective-permute-start.11
  290.1 8.6 collective-permute-start.11
  312.7 9.9 collective-permute-done.12
  324.9 145.6 %while.62 = (s32[]{:T(128)}, f32[128,5,128]{2,1,0:T(8,128)S(1)}, f32[128,1,1]{0,2,1:T(1,128)}, f32[2,128,5,128]{3,2,1,0:T(8,128)}, f32[128,1,128]{2,0,1:T(8,128)...) while((s32[]{:T(128)}, f32[128,5,128]{2,1,0:T(8,128)S(1)}, ...), condition=%wide.region_3.3_spmd, body=%wide.region_2.2_spmd.sunk | while | flops 8715235 | bytes 64688432 | solution.py:66
  376.6 8.6 collective-permute-start.11
  449.2 8.6 collective-permute-start.11
  471.8 10.2 collective-permute-done.12
  484.4 146.0 %while.62 = (s32[]{:T(128)}, f32[128,5,128]{2,1,0:T(8,128)S(1)}, f32[128,1,1]{0,2,1:T(1,128)}, f32[2,128,5,128]{3,2,1,0:T(8,128)}, f32[128,1,128]{2,0,1:T(8,128)...) while((s32[]{:T(128)}, f32[128,5,128]{2,1,0:T(8,128)S(1)}, ...), condition=%wide.region_3.3_spmd, body=%wide.region_2.2_spmd.sunk | while | flops 8715235 | bytes 64688432 | solution.py:66
  536.4 8.6 collective-permute-start.11
  609.1 8.6 collective-permute-start.11
  631.7 10.2 collective-permute-done.12
  644.2 146.0 %while.62 = (s32[]{:T(128)}, f32[128,5,128]{2,1,0:T(8,128)S(1)}, f32[128,1,1]{0,2,1:T(1,128)}, f32[2,128,5,128]{3,2,1,0:T(8,128)}, f32[128,1,128]{2,0,1:T(8,128)...) while((s32[]{:T(128)}, f32[128,5,128]{2,1,0:T(8,128)S(1)}, ...), condition=%wide.region_3.3_spmd, body=%wide.region_2.2_spmd.sunk | while | flops 8715235 | bytes 64688432 | solution.py:66
  768.9 8.6 collective-permute-start.11
  791.5 10.2 collective-permute-done.12
  804.1 146.0 %while.62 = (s32[]{:T(128)}, f32[128,5,128]{2,1,0:T(8,128)S(1)}, f32[128,1,1]{0,2,1:T(1,128)}, f32[2,128,5,128]{3,2,1,0:T(8,128)}, f32[128,1,128]{2,0,1:T(8,128)...) while((s32[]{:T(128)}, f32[128,5,128]{2,1,0:T(8,128)S(1)}, ...), condition=%wide.region_3.3_spmd, body=%wide.region_2.2_spmd.sunk | while | flops 8715235 | bytes 64688432 | solution.py:66
  856.1 8.6 collective-permute-start.11
  951.4 10.2 collective-permute-done.12
  963.9 146.0 %while.62 = (s32[]{:T(128)}, f32[128,5,128]{2,1,0:T(8,128)S(1)}, f32[128,1,1]{0,2,1:T(1,128)}, f32[2,128,5,128]{3,2,1,0:T(8,128)}, f32[128,1,128]{2,0,1:T(8,128)...) while((s32[]{:T(128)}, f32[128,5,128]{2,1,0:T(8,128)S(1)}, ...), condition=%wide.region_3.3_spmd, body=%wide.region_2.2_spmd.sunk | while | flops 8715235 | bytes 64688432 | solution.py:66
  1111.2 10.2 collective-permute-done.12
  1123.6 155.8 %while.61 = (s32[]{:T(128)}, f32[128,5,128]{2,1,0:T(8,128)S(1)}, f32[2,128,5,128]{3,2,1,0:T(8,128)}, f32[2,128,5,128]{3,2,1,0:T(8,128)}, f32[128,1,128]{2,0,1:T(...) while((s32[]{:T(128)}, f32[128,5,128]{2,1,0:T(8,128)S(1)}, ...), condition=%wide.region_6.7_spmd.clone, body=%wide.region_5.6_spmd.clone.sunk | while | flops 8715491 | bytes 66577184 | solution.py:66
  (1452 shorter events, 1148.4 us)
Async XLA Ops:
  166.6 15.3 %collective-permute-start.6 = (f32[16,5,128]{2,1,0:T(8,128)S(1)}, f32[16,5,128]{2,1,0:T(8,128)S(1)}, u32[]{:S(2)}, u32[]{:S(2)}) collective-permute-start(f32[16,5,128]{2,1,0:T(8,128)S(1)} %gather_fusion.9), channel_id=1, source_target_pairs={{1,0},{2,1},{3,2},{4,3},{5,4},{6,5},{7,6},{8,7},{9,8},{10,9},{11,1... | collective-permute-start | bytes 122888 | tf_op jit(solution)/shard_map/while/body/eval_jaxpr/while/body/eval_jaxpr/ppermute | solution.py:15
  217.4 12.8 collective-permute-start.11
  239.4 16.5 %collective-permute-start.6 = (f32[16,5,128]{2,1,0:T(8,128)S(1)}, f32[16,5,128]{2,1,0:T(8,128)S(1)}, u32[]{:S(2)}, u32[]{:S(2)}) collective-permute-start(f32[16,5,128]{2,1,0:T(8,128)S(1)} %gather_fusion.9), channel_id=1, source_target_pairs={{1,0},{2,1},{3,2},{4,3},{5,4},{6,5},{7,6},{8,7},{9,8},{10,9},{11,1... | collective-permute-start | bytes 122888 | tf_op jit(solution)/shard_map/while/body/eval_jaxpr/while/body/eval_jaxpr/ppermute | solution.py:15
  290.1 12.8 collective-permute-start.11
  325.5 15.3 %collective-permute-start.6 = (f32[16,5,128]{2,1,0:T(8,128)S(1)}, f32[16,5,128]{2,1,0:T(8,128)S(1)}, u32[]{:S(2)}, u32[]{:S(2)}) collective-permute-start(f32[16,5,128]{2,1,0:T(8,128)S(1)} %gather_fusion.9), channel_id=1, source_target_pairs={{1,0},{2,1},{3,2},{4,3},{5,4},{6,5},{7,6},{8,7},{9,8},{10,9},{11,1... | collective-permute-start | bytes 122888 | tf_op jit(solution)/shard_map/while/body/eval_jaxpr/while/body/eval_jaxpr/ppermute | solution.py:15
  376.6 12.8 collective-permute-start.11
  398.5 16.5 %collective-permute-start.6 = (f32[16,5,128]{2,1,0:T(8,128)S(1)}, f32[16,5,128]{2,1,0:T(8,128)S(1)}, u32[]{:S(2)}, u32[]{:S(2)}) collective-permute-start(f32[16,5,128]{2,1,0:T(8,128)S(1)} %gather_fusion.9), channel_id=1, source_target_pairs={{1,0},{2,1},{3,2},{4,3},{5,4},{6,5},{7,6},{8,7},{9,8},{10,9},{11,1... | collective-permute-start | bytes 122888 | tf_op jit(solution)/shard_map/while/body/eval_jaxpr/while/body/eval_jaxpr/ppermute | solution.py:15
  449.2 12.8 collective-permute-start.11
  485.0 15.6 %collective-permute-start.6 = (f32[16,5,128]{2,1,0:T(8,128)S(1)}, f32[16,5,128]{2,1,0:T(8,128)S(1)}, u32[]{:S(2)}, u32[]{:S(2)}) collective-permute-start(f32[16,5,128]{2,1,0:T(8,128)S(1)} %gather_fusion.9), channel_id=1, source_target_pairs={{1,0},{2,1},{3,2},{4,3},{5,4},{6,5},{7,6},{8,7},{9,8},{10,9},{11,1... | collective-permute-start | bytes 122888 | tf_op jit(solution)/shard_map/while/body/eval_jaxpr/while/body/eval_jaxpr/ppermute | solution.py:15
  536.4 12.8 collective-permute-start.11
  558.3 16.5 %collective-permute-start.6 = (f32[16,5,128]{2,1,0:T(8,128)S(1)}, f32[16,5,128]{2,1,0:T(8,128)S(1)}, u32[]{:S(2)}, u32[]{:S(2)}) collective-permute-start(f32[16,5,128]{2,1,0:T(8,128)S(1)} %gather_fusion.9), channel_id=1, source_target_pairs={{1,0},{2,1},{3,2},{4,3},{5,4},{6,5},{7,6},{8,7},{9,8},{10,9},{11,1... | collective-permute-start | bytes 122888 | tf_op jit(solution)/shard_map/while/body/eval_jaxpr/while/body/eval_jaxpr/ppermute | solution.py:15
  609.1 12.8 collective-permute-start.11
  644.8 15.6 %collective-permute-start.6 = (f32[16,5,128]{2,1,0:T(8,128)S(1)}, f32[16,5,128]{2,1,0:T(8,128)S(1)}, u32[]{:S(2)}, u32[]{:S(2)}) collective-permute-start(f32[16,5,128]{2,1,0:T(8,128)S(1)} %gather_fusion.9), channel_id=1, source_target_pairs={{1,0},{2,1},{3,2},{4,3},{5,4},{6,5},{7,6},{8,7},{9,8},{10,9},{11,1... | collective-permute-start | bytes 122888 | tf_op jit(solution)/shard_map/while/body/eval_jaxpr/while/body/eval_jaxpr/ppermute | solution.py:15
  696.3 12.8 collective-permute-start.11
  718.2 16.5 %collective-permute-start.6 = (f32[16,5,128]{2,1,0:T(8,128)S(1)}, f32[16,5,128]{2,1,0:T(8,128)S(1)}, u32[]{:S(2)}, u32[]{:S(2)}) collective-permute-start(f32[16,5,128]{2,1,0:T(8,128)S(1)} %gather_fusion.9), channel_id=1, source_target_pairs={{1,0},{2,1},{3,2},{4,3},{5,4},{6,5},{7,6},{8,7},{9,8},{10,9},{11,1... | collective-permute-start | bytes 122888 | tf_op jit(solution)/shard_map/while/body/eval_jaxpr/while/body/eval_jaxpr/ppermute | solution.py:15
  768.9 12.8 collective-permute-start.11
  804.7 15.6 %collective-permute-start.6 = (f32[16,5,128]{2,1,0:T(8,128)S(1)}, f32[16,5,128]{2,1,0:T(8,128)S(1)}, u32[]{:S(2)}, u32[]{:S(2)}) collective-permute-start(f32[16,5,128]{2,1,0:T(8,128)S(1)} %gather_fusion.9), channel_id=1, source_target_pairs={{1,0},{2,1},{3,2},{4,3},{5,4},{6,5},{7,6},{8,7},{9,8},{10,9},{11,1... | collective-permute-start | bytes 122888 | tf_op jit(solution)/shard_map/while/body/eval_jaxpr/while/body/eval_jaxpr/ppermute | solution.py:15
  878.0 16.5 %collective-permute-start.6 = (f32[16,5,128]{2,1,0:T(8,128)S(1)}, f32[16,5,128]{2,1,0:T(8,128)S(1)}, u32[]{:S(2)}, u32[]{:S(2)}) collective-permute-start(f32[16,5,128]{2,1,0:T(8,128)S(1)} %gather_fusion.9), channel_id=1, source_target_pairs={{1,0},{2,1},{3,2},{4,3},{5,4},{6,5},{7,6},{8,7},{9,8},{10,9},{11,1... | collective-permute-start | bytes 122888 | tf_op jit(solution)/shard_map/while/body/eval_jaxpr/while/body/eval_jaxpr/ppermute | solution.py:15
  964.5 15.6 %collective-permute-start.6 = (f32[16,5,128]{2,1,0:T(8,128)S(1)}, f32[16,5,128]{2,1,0:T(8,128)S(1)}, u32[]{:S(2)}, u32[]{:S(2)}) collective-permute-start(f32[16,5,128]{2,1,0:T(8,128)S(1)} %gather_fusion.9), channel_id=1, source_target_pairs={{1,0},{2,1},{3,2},{4,3},{5,4},{6,5},{7,6},{8,7},{9,8},{10,9},{11,1... | collective-permute-start | bytes 122888 | tf_op jit(solution)/shard_map/while/body/eval_jaxpr/while/body/eval_jaxpr/ppermute | solution.py:15
  1037.9 16.5 %collective-permute-start.6 = (f32[16,5,128]{2,1,0:T(8,128)S(1)}, f32[16,5,128]{2,1,0:T(8,128)S(1)}, u32[]{:S(2)}, u32[]{:S(2)}) collective-permute-start(f32[16,5,128]{2,1,0:T(8,128)S(1)} %gather_fusion.9), channel_id=1, source_target_pairs={{1,0},{2,1},{3,2},{4,3},{5,4},{6,5},{7,6},{8,7},{9,8},{10,9},{11,1... | collective-permute-start | bytes 122888 | tf_op jit(solution)/shard_map/while/body/eval_jaxpr/while/body/eval_jaxpr/ppermute | solution.py:15
  1124.8 16.2 %collective-permute-start = (f32[16,5,128]{2,1,0:T(8,128)}, f32[16,5,128]{2,1,0:T(8,128)S(1)}, u32[]{:S(2)}, u32[]{:S(2)}) collective-permute-start(f32[16,5,128]{2,1,0:T(8,128)} %gather_fusion), channel_id=1, source_target_pairs={{1,0},{2,1},{3,2},{4,3},{5,4},{6,5},{7,6},{8,7},{9,8},{10,9},{11,1... | collective-permute-start | bytes 122888 | tf_op jit(solution)/shard_map/while/body/eval_jaxpr/ppermute | solution.py:15
  1179.0 12.9 collective-permute-start.5
  1203.0 17.1 %collective-permute-start = (f32[16,5,128]{2,1,0:T(8,128)}, f32[16,5,128]{2,1,0:T(8,128)S(1)}, u32[]{:S(2)}, u32[]{:S(2)}) collective-permute-start(f32[16,5,128]{2,1,0:T(8,128)} %gather_fusion), channel_id=1, source_target_pairs={{1,0},{2,1},{3,2},{4,3},{5,4},{6,5},{7,6},{8,7},{9,8},{10,9},{11,1... | collective-permute-start | bytes 122888 | tf_op jit(solution)/shard_map/while/body/eval_jaxpr/ppermute | solution.py:15
  1256.6 12.9 collective-permute-start.5
  (452 other events, 2597.5 us)
where the time goes:
time: 1320 us; the launch traced here: 1300 us
  starting transfers between devices  477 us (36%)
  local copies, waits for them, and re-layouts  369 us (28%)
  other arithmetic  336 us (25%)
  waiting for transfers between devices  106 us (8%)
    ppermute x103, starting transfers between devices, from_behind(): lax.ppermute(value, axis, [(source, source + steps) for source in range(f...  471 us
    gather x48, local copies, waits for them, and re-layouts, operate(): gathered = extended[neighbours]  174 us
    dot_general x48, other arithmetic, operate(): jnp.einsum('bnc,bnkc->bkc', face_coef, gathered, precision=highest)  133 us
    ppermute x103, waiting for transfers between devices, from_behind(): lax.ppermute(value, axis, [(source, source + steps) for source in range(f...  102 us
    dot_general x48, other arithmetic, operate(): own = jnp.einsum('bijc,bic->bjc', jac, field, precision=highest)  96.4 us
    gather x48, local copies, waits for them, and re-layouts, operate(): from_lower = from_behind(field[to_higher], 'space', 1)  75.9 us
    gather x48, local copies, waits for them, and re-layouts, operate(): from_higher = from_behind(field[to_lower], 'space', -1)  61.4 us
    mul x48, other arithmetic, level_step(): field = live * (field + precond * (rhs - operate(field, jac)))  49.9 us
  transfers between devices with their start and end apart: 104, of which 33 were waited for; matrix products, arithmetic and copies ran while one was open for 12% of the time, Pallas kernels for 0%

commit v1 on v0

v1 whole, which is shorter than its diff:
```python
import functools

import jax
import jax.numpy as jnp
from jax import lax
from jax.experimental import pallas as pl
from jax.experimental.pallas import tpu as pltpu
from jax.sharding import PartitionSpec as P

ITERS = 3
STEPS = 2
SWEEPS = ITERS * STEPS
SLOTS = 3
CHUNKS = 4
INVERSE_STEP = 6.0
MESH = pl.DeviceIdType.MESH
F32 = jnp.float32


def kernel(
    src_h, term_h, jac_h, face_h, cell_h, nbr, snd, live_s, vol_h, shape_h, w_s,
    adj_o, sens_o,
    K, SRC, F, CL, CR, VOL, SH, LP, LPM, R, XIN, XB, YB, CB, LPB, E0, E1, E2,
    SLO, SHI, OUT, ACC, RED, PART, TOT,
    ld, xr, elo, ehi, slo, shi, osem, hsem, psr, pss, fss, fsr,
):
    comp, nb, cells = XIN.shape
    nei = F.shape[0]
    halo = SLO.shape[1]
    groups = nb // 8
    tm = lax.axis_index("tm")
    d = lax.axis_index("space")
    n_tm = lax.axis_size("tm")
    n_sp = lax.axis_size("space")
    has_lo, has_hi = d > 0, d < n_sp - 1
    first, last = tm == n_tm - 1, tm == 0
    E = (E0, E1, E2)
    lo, hi = d - 1, d + 1
    XR, YR, CRW, LPR = (ref.reshape(ref.shape[0] * 8, cells) for ref in (XB, YB, CB, LPB))

    loads = [
        pltpu.make_async_copy(jac_h.at[0], K, ld.at[0]),
        pltpu.make_async_copy(face_h, F, ld.at[1]),
        pltpu.make_async_copy(cell_h, CL, ld.at[2]),
        pltpu.make_async_copy(vol_h, VOL, ld.at[3]),
        pltpu.make_async_copy(src_h, SRC, ld.at[4]),
        pltpu.make_async_copy(shape_h, SH, ld.at[5]),
    ]
    for copy in loads:
        copy.start()
    term_copy = pltpu.make_async_copy(term_h, XIN, ld.at[6])

    @pl.when(first)
    def _():
        term_copy.start()

    barrier = pltpu.get_barrier_semaphore()
    for dt in (-1, 0, 1):
        for ds in (-1, 0, 1):
            if dt == 0 and ds == 0:
                continue
            ok = jnp.logical_and(
                jnp.logical_and(tm + dt >= 0, tm + dt < n_tm),
                jnp.logical_and(d + ds >= 0, d + ds < n_sp),
            )

            @pl.when(ok)
            def _():
                pl.semaphore_signal(barrier, 1, device_id=(tm + dt, d + ds), device_id_type=MESH)

    @pl.when(last)
    def _():
        for row in range(2, n_tm):
            pl.semaphore_signal(barrier, 1, device_id=(row, d), device_id_type=MESH)

    @pl.when(tm >= 2)
    def _():
        pl.semaphore_signal(barrier, 1, device_id=(0, d), device_id_type=MESH)

    zero = jnp.zeros((comp, cells), F32)
    for e in E:

        def clear(i, _):
            for u in range(8):
                e[i * 8 + u] = zero
            return 0

        lax.fori_loop(0, nb // 8, clear, 0)
        e[nb + 2 * halo] = zero

        @pl.when(jnp.logical_not(has_lo))
        def _():
            for s in range(halo):
                e[nb + s] = zero

        @pl.when(jnp.logical_not(has_hi))
        def _():
            for s in range(halo):
                e[nb + halo + s] = zero

    for s in range(2 * halo + 1):
        XB[nb + s] = jnp.zeros((8, cells), F32)

    for copy in loads[:4]:
        copy.wait()

    lc = live_s[0]
    lane = lax.broadcasted_iota(jnp.int32, (8, cells), 1)
    sub = lax.broadcasted_iota(jnp.int32, (8, cells), 0)

    def prepare(g, _):
        rows = pl.ds(pl.multiple_of(g * 8, 8), 8)
        mass = INVERSE_STEP * VOL[rows, :]
        cell = CL[rows, :]
        fsum = F[0, rows, :]
        for k in range(1, nei):
            fsum = fsum + F[k, rows, :]
        CR[rows, :] = jnp.where(lane == cells - 1, 0.0, cell)
        CL[rows, :] = jnp.where(lane == 0, 0.0, cell)
        live = jnp.where(sub + g * 8 < lc, 1.0, 0.0)
        for j in range(comp):
            lp = live / (mass + K[j, j, rows, :] + fsum + 2.0 * cell)
            lpm = lp * mass
            LP[j, rows, :] = lp
            LPM[j, rows, :] = lpm
            LPR[pl.ds(g * 64 + j, 8, stride=8), :] = lp
            for i in range(comp):
                k_ij = -lp * K[i, j, rows, :]
                if i == j:
                    k_ij = k_ij + (live - lpm)
                K[i, j, rows, :] = k_ij
        return 0

    lax.fori_loop(0, groups, prepare, 0)

    partners = (
        jnp.where(has_lo, 1, 0) + jnp.where(has_hi, 1, 0)
    )
    rows_near = jnp.where(first, 0, 1) + jnp.where(last, 0, 1)
    expect = partners + rows_near * (1 + partners)
    expect = expect + jnp.where(last, n_tm - 2, 0) + jnp.where(tm >= 2, 1, 0)
    pl.semaphore_wait(barrier, expect)

    def halo_copy(side, slot, buf, row):
        if side == 0:
            return pltpu.make_async_remote_copy(
                SLO.at[buf], E[slot].at[pl.ds(nb + halo, halo)], slo.at[buf], ehi.at[slot],
                device_id=(row, lo), device_id_type=MESH)
        return pltpu.make_async_remote_copy(
            SHI.at[buf], E[slot].at[pl.ds(nb, halo)], shi.at[buf], elo.at[slot],
            device_id=(row, hi), device_id_type=MESH)

    def start_side(side, slot, buf, row, cond):
        @pl.when(cond)
        def _():
            halo_copy(side, slot, buf, row).start()

    def state_copy(c):
        rows = pl.ds(c * (nb // CHUNKS), nb // CHUNKS)
        return pltpu.make_async_remote_copy(
            OUT.at[0, :, rows], XIN.at[:, rows], hsem.at[c], xr.at[c],
            device_id=(tm - 1, d), device_id_type=MESH)

    @pl.when(first)
    def _():
        term_copy.wait()

    @pl.when(jnp.logical_not(first))
    def _():
        for c in range(CHUNKS):
            state_copy(c).wait_recv()

    def spread(g, _):
        rows = pl.ds(pl.multiple_of(g * 8, 8), 8)
        keep = jnp.where(sub + g * 8 < lc, 1.0, 0.0)
        for j in range(comp):
            XR[pl.ds(g * 64 + j, 8, stride=8), :] = keep * XIN[j, rows, :]
        return 0

    lax.fori_loop(0, groups, spread, 0)

    @pl.when(first)
    def _():
        for side, buf in ((0, SLO), (1, SHI)):
            for s in range(halo):
                buf[1, s] = XB[snd[side, s]][:comp]
        start_side(0, 0, 1, tm, has_lo)
        start_side(1, 0, 1, tm, has_hi)

    loads[4].wait()
    loads[5].wait()

    for it in range(SWEEPS):
        level = STEPS - 1 - it // ITERS
        sweep = it % ITERS
        slot = it % SLOTS
        buf = it % 2

        def gather_local(g, _):
            for u in range(8):
                b = g * 8 + u
                c = None
                for k in range(nei):
                    t = F[k, pl.ds(b, 1), :] * XB[nbr[k, b]]
                    c = t if c is None else c + t
                CB[b] = c
            return 0

        lax.fori_loop(0, groups, gather_local, 0)

        def own(g, _):
            rows = pl.ds(pl.multiple_of(g * 8, 8), 8)
            xs = [XR[pl.ds(g * 64 + j, 8, stride=8), :] for j in range(comp)]
            cl, cr = CL[rows, :], CR[rows, :]
            for j in range(comp):
                lp = LP[j, rows, :]
                if sweep == 0:
                    y = lp * SRC[level, j, rows, :] + LPM[j, rows, :] * xs[j]
                    R[j, rows, :] = y
                else:
                    y = R[j, rows, :]
                for i in range(comp):
                    y = y + K[i, j, rows, :] * xs[i]
                beside = cl * pltpu.roll(xs[j], 1, 1) + cr * pltpu.roll(xs[j], cells - 1, 1)
                y = y + lp * (CRW[pl.ds(g * 64 + j, 8, stride=8), :] + beside)
                YR[pl.ds(g * 64 + j, 8, stride=8), :] = y
            return 0

        lax.fori_loop(0, groups, own, 0)

        if it >= 2:
            @pl.when(has_lo)
            def _():
                halo_copy(0, 0, buf, tm).wait_send()

            @pl.when(has_hi)
            def _():
                halo_copy(1, 0, buf, tm).wait_send()
        if it == 1:
            @pl.when(jnp.logical_and(first, has_lo))
            def _():
                halo_copy(0, 0, buf, tm).wait_send()

            @pl.when(jnp.logical_and(first, has_hi))
            def _():
                halo_copy(1, 0, buf, tm).wait_send()

        @pl.when(has_hi)
        def _():
            halo_copy(0, slot, buf, tm).wait_recv()

        @pl.when(has_lo)
        def _():
            halo_copy(1, slot, buf, tm).wait_recv()

        e = E[slot]

        def finish(b):
            c = None
            for k in range(nei):
                t = F[k, b][None, :] * e[nbr[k, b]]
                c = t if c is None else c + t
            return YB[b][:comp] + LPB[b][:comp] * c

        final = it == SWEEPS - 1
        if final:
            row, after = tm - 1, 0
            go_lo = jnp.logical_and(has_lo, jnp.logical_not(last))
            go_hi = jnp.logical_and(has_hi, jnp.logical_not(last))
        else:
            row, after = tm, (it + 1) % SLOTS
            go_lo, go_hi = has_lo, has_hi
        for side, store, go in ((0, SLO, go_lo), (1, SHI, go_hi)):
            for s in range(halo):
                store[buf, s] = finish(snd[side, s])
            start_side(side, after, buf, row, go)

        def post(g, _):
            for u in range(8):
                b = g * 8 + u
                XB[b, pl.ds(0, comp), :] = finish(b)
            return 0

        if sweep < ITERS - 1:
            lax.fori_loop(0, groups, post, 0)
            continue

        w = w_s[level]

        def post_level(g, _):
            post(g, 0)
            rows = pl.ds(pl.multiple_of(g * 8, 8), 8)
            acc = None
            for j in range(comp):
                x = XR[pl.ds(g * 64 + j, 8, stride=8), :]
                OUT[level, j, rows, :] = x
                t = x * SH[j, rows, :]
                acc = t if acc is None else acc + t
            acc = w * acc
            if it > ITERS:
                acc = ACC[rows, :] + acc
            ACC[rows, :] = acc
            return 0

        if not final:
            lax.fori_loop(0, groups, post_level, 0)
        else:
            for c in range(CHUNKS):
                lax.fori_loop(c * groups // CHUNKS, (c + 1) * groups // CHUNKS, post_level, 0)

                @pl.when(jnp.logical_not(last))
                def _():
                    state_copy(c).start()

        pltpu.make_async_copy(OUT.at[level], adj_o.at[level], osem.at[level]).start()

    PART[...] = jnp.sum(ACC[...].T, axis=0, keepdims=True)

    def part_copy():
        return pltpu.make_async_remote_copy(
            PART, RED, pss, psr, device_id=(tm - 1, d), device_id_type=MESH)

    @pl.when(jnp.logical_not(first))
    def _():
        part_copy().wait_recv()
        PART[...] = PART[...] + RED[...]

    @pl.when(jnp.logical_not(last))
    def _():
        part_copy().start()

    def total_copy(row):
        return pltpu.make_async_remote_copy(
            PART, TOT, fss.at[row], fsr, device_id=(row, d), device_id_type=MESH)

    @pl.when(last)
    def _():
        for row in range(1, n_tm):
            total_copy(row).start()
        sens_o[...] = PART[...]
        for row in range(1, n_tm):
            total_copy(row).wait_send()

    @pl.when(jnp.logical_not(last))
    def _():
        for c in range(CHUNKS):
            state_copy(c).wait_send()
        part_copy().wait_send()
        total_copy(0).wait_recv()
        sens_o[...] = TOT[...]

    inner = (SWEEPS - 2) % 2
    outer = (SWEEPS - 1) % 2
    for side, has in ((0, has_lo), (1, has_hi)):
        @pl.when(has)
        def _():
            halo_copy(side, 0, inner, tm).wait_send()

        @pl.when(jnp.logical_and(has, jnp.logical_not(last)))
        def _():
            halo_copy(side, 0, outer, tm).wait_send()
    for level in range(STEPS):
        pltpu.make_async_copy(OUT.at[level], adj_o.at[level], osem.at[level]).wait()


def per_device(source, terminal, jacobian, face_coef, cell_coef, neighbours, send_blocks,
               live_count, volume, shape_field, weights):
    nb, comp, cells = terminal.shape
    nei = face_coef.shape[1]
    halo = send_blocks.shape[2]
    anys = pl.BlockSpec(memory_space=pl.ANY)
    smem = pl.BlockSpec(memory_space=pltpu.SMEM)
    vmem = pltpu.VMEM
    dma = pltpu.SemaphoreType.DMA
    table = nb + 2 * halo + 1
    adj, sens = pl.pallas_call(
        kernel,
        out_shape=(
            jax.ShapeDtypeStruct((STEPS, comp, nb, cells), F32),
            jax.ShapeDtypeStruct((1, nb), F32),
        ),
        in_specs=[anys, anys, anys, anys, anys, smem, smem, smem, anys, anys, smem],
        out_specs=(anys, pl.BlockSpec(memory_space=pltpu.VMEM)),
        scratch_shapes=[
            vmem((comp, comp, nb, cells), F32),
            vmem((STEPS, comp, nb, cells), F32),
            vmem((nei, nb, cells), F32),
            vmem((nb, cells), F32),
            vmem((nb, cells), F32),
            vmem((nb, cells), F32),
            vmem((comp, nb, cells), F32),
            vmem((comp, nb, cells), F32),
            vmem((comp, nb, cells), F32),
            vmem((comp, nb, cells), F32),
            vmem((comp, nb, cells), F32),
            vmem((table, 8, cells), F32),
            vmem((nb, 8, cells), F32),
            vmem((nb, 8, cells), F32),
            vmem((nb, 8, cells), F32),
            vmem((table, comp, cells), F32),
            vmem((table, comp, cells), F32),
            vmem((table, comp, cells), F32),
            vmem((2, halo, comp, cells), F32),
            vmem((2, halo, comp, cells), F32),
            vmem((STEPS, comp, nb, cells), F32),
            vmem((nb, cells), F32),
            vmem((1, nb), F32),
            vmem((1, nb), F32),
            vmem((1, nb), F32),
            dma((7,)),
            dma((CHUNKS,)),
            dma((SLOTS,)),
            dma((SLOTS,)),
            dma((2,)),
            dma((2,)),
            dma((STEPS,)),
            dma((CHUNKS,)),
            dma(()),
            dma(()),
            dma((lax.axis_size("tm"),)),
            dma(()),
        ],
        compiler_params=pltpu.CompilerParams(collective_id=0, has_side_effects=True),
        name="sweep",
    )(
        source.transpose(0, 2, 1, 3),
        terminal.transpose(1, 0, 2),
        jacobian.transpose(0, 2, 3, 1, 4),
        face_coef.transpose(1, 0, 2),
        cell_coef,
        neighbours.T,
        send_blocks[0],
        live_count,
        volume,
        shape_field.transpose(1, 0, 2),
        weights,
    )
    return adj.transpose(0, 2, 1, 3), sens.reshape(nb)


def solution(mesh):
    return jax.shard_map(
        per_device,
        mesh=mesh,
        in_specs=(
            P("tm", "space", None, None),
            P("space", None, None),
            P("tm", "space", None, None, None),
            P("space", None, None),
            P("space", None),
            P("space", None),
            P("space", None, None),
            P("space"),
            P("space", None),
            P("space", None, None),
            P("tm"),
        ),
        out_specs=(P("tm", "space", None, None), P("space")),
        check_vma=False,
    )
```

time: 1320 us -> 279 us (0.21); the launches traced: 1300 us -> 276 us
  starting transfers between devices: 477 us -> 0 us
  local copies, waits for them, and re-layouts: 369 us -> 3.14 us
  other arithmetic: 336 us -> 0 us
  Pallas kernels: 0 us -> 272 us
  waiting for transfers between devices: 106 us -> 0 us
    ppermute x103 -> x0, starting transfers between devices: 471 us -> none  [from_behind(): lax.ppermute(value, axis, [(source, source + steps) for source in range(f...]
    gather x144 -> x0, local copies, waits for them, and re-layouts: 312 us -> none  [the longest x48 174 us: operate(): gathered = extended[neighbours]]
    pallas_call x0 -> x1, Pallas kernels: none -> 272 us  [per_device(): pl.pallas_call(kernel, out_shape=(jax.ShapeDtypeStruct((STEPS, comp, nb,...]
    dot_general x96 -> x0, other arithmetic: 230 us -> none  [the longest x48 133 us: operate(): jnp.einsum('bnc,bnkc->bkc', face_coef, gathered, precision=highest)]
    ppermute x103 -> x0, waiting for transfers between devices: 102 us -> none  [from_behind(): lax.ppermute(value, axis, [(source, source + steps) for source in range(f...]
    mul x50 -> x0, other arithmetic: 50.2 us -> none  [the longest x48 49.9 us: level_step(): field = live * (field + precond * (rhs - operate(field, jac)))]
    while x748 -> x0, local copies, waits for them, and re-layouts: 38.7 us -> none
    concatenate x48 -> x0, other arithmetic: 31.5 us -> none  [operate(): extended = jnp.concatenate([field, from_lower, from_higher, blank], axis=0)]
  transfers between devices with their start and end apart: 104 -> 0, of which waited for: 33 -> 0; matrix products, arithmetic and copies ran while one was open for 12% -> 0% of each run, Pallas kernels for 0% -> 0%
where the time goes in v1:
time: 279 us; the launch traced here: 276 us
  Pallas kernels  272 us (97%)
  local copies, waits for them, and re-layouts  3.14 us (1%)
    pallas_call x1, Pallas kernels, per_device(): pl.pallas_call(kernel, out_shape=(jax.ShapeDtypeStruct((STEPS, comp, nb,...  272 us

profile of v1, /device:TPU:96, one launch (start us, length us, event | category | flops | bytes accessed | tf_op | source)
XLA Modules:
  0.0 276.2 jit_solution(429892819858515923)
XLA Ops:
  1.3 271.7 %sweep.1 = (f32[2,5,128,128]{3,2,1,0:T(8,128)}, f32[1,128]{1,0:T(1,128)}) custom-call(f32[2,5,128,128]{3,2,1,0:T(8,128)} %bitcast.11, f32[5,128,128]{2,1,0:T(8,128)} %bitcast.13, f32[1,5,5,128,128]{4,3,2,1,0:T(8,128)} %bitcast.9, f32[6,128,128]{2,1,0:T(8,128)} %bitcast.12, f32[128,128]{1,0:T(8,128)} %cell_h.1, s32[6,128]{1,0:T(8,128)} %bitcast.15, ...), custom_call_target="tpu_custom_call" | custom-call | tf_op jit(solution)/shard_map/sweep/pallas_call | solution.py:376
  273.0 2.0 copy.16
  275.0 1.2 copy.17

commit v2 on v0

v2 whole, which is shorter than its diff:
```python
import functools

import jax
import jax.numpy as jnp
from jax import lax
from jax.experimental import pallas as pl
from jax.experimental.pallas import tpu as pltpu
from jax.sharding import PartitionSpec as P

ITERS = 3
STEPS = 2
SWEEPS = ITERS * STEPS
SLOTS = 3
CHUNKS = 4
PIECES = 3
INVERSE_STEP = 6.0
MESH = pl.DeviceIdType.MESH
F32 = jnp.float32


def both(*conds):
    return functools.reduce(jnp.logical_and, conds)


def kernel(
    src_h, term_h, jac_h, face_h, cell_h, ints_h, vol_h, shape_h, w_s,
    adj_o, sens_o,
    KA, KB, SRCA, SRCB, F, CELL, CL, CR, VOL, SH, LPA, LPB, LPMA, LPMB, LBA, LBB,
    R, XIN, XB, YB, E0, E1, E2, SLO, SHI, OUTA, OUTB, ACC, RED, PART, TOT,
    WOUT, WA, WB, IV, INTS, FH, LHA, LHB, NH,
    ra, rb, sa, rc, sc, isem, xr, elo, ehi, slo, shi, oas, obs, ors, hsem, psr, pss, fss, fsr,
):
    comp, nb, cells = XIN.shape
    nei = F.shape[0]
    halo = SLO.shape[1]
    groups = nb // 8
    tm = lax.axis_index("tm")
    d = lax.axis_index("space")
    n_tm = lax.axis_size("tm")
    n_sp = lax.axis_size("space")

    x, z, c = tm // 2, d // 4, d % 2
    y = (d // 2) % 2 * 2 + tm % 2

    def path(k, q):
        qz, j = q // 4, q % 4
        qy = jnp.where(qz % 2 == 0, j, 3 - j)
        return 2 * k + qy % 2, 4 * qz + qy // 2 * 2 + 1

    n_planes = n_tm // 2
    native = x == n_planes - 1
    onpath = both(jnp.logical_not(native), c == 1)
    active = jnp.logical_or(native, onpath)
    p = jnp.where(native, d, 4 * z + jnp.where(z % 2 == 0, y, 3 - y))
    first = tm == n_tm - 1
    last = both(onpath, x == 0)
    more = both(active, jnp.logical_not(last))
    later = both(active, jnp.logical_not(first))
    has_lo, has_hi = p > 0, p < n_sp - 1

    def pick(cond, a, b):
        return jnp.where(cond, a[0], b[0]), jnp.where(cond, a[1], b[1])

    def same(dev):
        return both(dev[0] == tm, dev[1] == d)

    def peer(q):
        return pick(native, (tm, q), path(x, q))

    def next_dev(q):
        return pick(first, (tm - 1, q), pick(native, path(x - 1, q), path(jnp.maximum(x - 1, 0), q)))

    def prev_dev(q):
        return pick(native, (tm + 1, q), pick(x == n_planes - 2, (n_tm - 2, q), path(x + 1, q)))

    lo, hi = peer(p - 1), peer(p + 1)
    nxt = next_dev(p)
    nlo, nhi = next_dev(p - 1), next_dev(p + 1)
    home_a, home_b = (2 * x + 1, p), (2 * x, p)
    self_a = same(home_a)
    mover = jnp.logical_not(native)
    worker = path(x, d)
    own_worker = same(worker)
    odd = tm % 2 == 1
    summer = path(0, d)
    own_summer = same(summer)

    def remote(src, dst, ssem, rsem, dev):
        return pltpu.make_async_remote_copy(src, dst, ssem, rsem, device_id=dev, device_id_type=MESH)

    local = [
        pltpu.make_async_copy(face_h, F, rc.at[0]),
        pltpu.make_async_copy(cell_h, CELL, rc.at[1]),
        pltpu.make_async_copy(vol_h, VOL, rc.at[2]),
        pltpu.make_async_copy(shape_h, SH, rc.at[3]),
        pltpu.make_async_copy(ints_h, INTS, isem),
        pltpu.make_async_copy(jac_h.at[0], KB, rb.at[0]),
        pltpu.make_async_copy(src_h, SRCB, rb.at[1]),
    ]

    @pl.when(native)
    def _():
        for copy in local:
            copy.start()

    term_copy = pltpu.make_async_copy(term_h, XIN, xr.at[0])

    @pl.when(first)
    def _():
        term_copy.start()

    barrier = pltpu.get_barrier_semaphore()
    edges = [(both(active, has_lo), lo), (both(active, has_hi), hi)]
    for ds in (-1, 0, 1):
        inside = both(p + ds >= 0, p + ds < n_sp)
        edges.append((both(more, inside), next_dev(p + ds)))
        edges.append((both(later, inside), prev_dev(p + ds)))
    edges.append((both(mover, jnp.logical_not(own_worker)), worker))
    edges.append((both(onpath, jnp.logical_not(self_a)), home_a))
    edges.append((onpath, home_b))
    for t in range(n_tm):
        edges.append((both(last, jnp.logical_not(same((t, p)))), (t, p)))
    edges.append((jnp.logical_not(own_summer), summer))
    expect = 0
    for cond, dev in edges:

        @pl.when(cond)
        def _():
            pl.semaphore_signal(barrier, 1, device_id=dev, device_id_type=MESH)

        expect = expect + jnp.where(cond, 1, 0)

    for level in range(STEPS):
        WOUT[level] = jnp.full((1, cells), w_s[level], F32)

        @pl.when(native)
        def _():
            WB[level] = jnp.full((1, cells), w_s[level], F32)

    pl.semaphore_wait(barrier, expect)

    def coefficients(dev):
        return [
            remote(ints_h, IV, sc.at[4], rc.at[4], dev),
            remote(face_h, F, sc.at[0], rc.at[0], dev),
            remote(cell_h, CELL, sc.at[1], rc.at[1], dev),
            remote(vol_h, VOL, sc.at[2], rc.at[2], dev),
            remote(shape_h, SH, sc.at[3], rc.at[3], dev),
        ]

    def slab_operands(K, SRC, W, sems, dev):
        return [
            remote(jac_h.at[0], K, sa.at[0], sems.at[0], dev),
            remote(src_h, SRC, sa.at[1], sems.at[1], dev),
            remote(WOUT, W, sa.at[2], sems.at[2], dev),
        ]

    self_operands = [
        pltpu.make_async_copy(jac_h.at[0], KA, ra.at[0]),
        pltpu.make_async_copy(src_h, SRCA, ra.at[1]),
    ]

    @pl.when(both(mover, odd, jnp.logical_not(own_worker)))
    def _():
        for copy in slab_operands(KA, SRCA, WA, ra, worker):
            copy.start()

    @pl.when(both(mover, odd, own_worker))
    def _():
        for copy in self_operands:
            copy.start()
        WA[...] = WOUT[...]

    @pl.when(both(mover, jnp.logical_not(odd)))
    def _():
        for copy in coefficients(worker):
            copy.start()
        for copy in slab_operands(KB, SRCB, WB, rb, worker):
            copy.start()

    E = (E0, E1, E2)
    XR, YR, LAR, LBR = (ref.reshape(ref.shape[0] * 8, cells) for ref in (XB, YB, LBA, LBB))
    lane = lax.broadcasted_iota(jnp.int32, (8, cells), 1)
    sub = lax.broadcasted_iota(jnp.int32, (8, cells), 0)
    sends = nei * nb

    def halo_copy(side, slot, buf, dev):
        if side == 0:
            return remote(SLO.at[buf], E[slot].at[pl.ds(nb + halo, halo)], slo.at[buf], ehi.at[slot], dev)
        return remote(SHI.at[buf], E[slot].at[pl.ds(nb, halo)], shi.at[buf], elo.at[slot], dev)

    def start_side(side, slot, buf, dev, cond):
        @pl.when(cond)
        def _():
            halo_copy(side, slot, buf, dev).start()

    def state_copy(i):
        rows = pl.ds(i * (nb // CHUNKS), nb // CHUNKS)
        return remote(OUTB.at[0, :, rows], XIN.at[:, rows], hsem.at[i], xr.at[i], nxt)

    def halo_tables():
        for s in range(2 * halo):
            b = INTS[sends + s]
            for k in range(nei):
                NH[s * nei + k] = INTS[k * nb + b]
                FH[k, pl.ds(s, 1), :] = F[k, b][None, :]

    def prepare_slab(K, LP, LPM, LB, LPR, LH):
        lc = INTS[sends + 2 * halo]

        def prepare(g, _):
            rows = pl.ds(pl.multiple_of(g * 8, 8), 8)
            mass = INVERSE_STEP * VOL[rows, :]
            cell = CELL[rows, :]
            fsum = F[0, rows, :]
            for k in range(1, nei):
                fsum = fsum + F[k, rows, :]
            CR[rows, :] = jnp.where(lane == cells - 1, 0.0, cell)
            CL[rows, :] = jnp.where(lane == 0, 0.0, cell)
            live = jnp.where(sub + g * 8 < lc, 1.0, 0.0)
            for j in range(comp):
                lp = live / (mass + K[j, j, rows, :] + fsum + 2.0 * cell)
                lpm = lp * mass
                LP[j, rows, :] = lp
                LPM[j, rows, :] = lpm
                LPR[pl.ds(g * 64 + j, 8, stride=8), :] = lp
                for i in range(comp):
                    k_ij = -lp * K[i, j, rows, :]
                    if i == j:
                        k_ij = k_ij + (live - lpm)
                    K[i, j, rows, :] = k_ij
            return 0

        lax.fori_loop(0, groups, prepare, 0)
        for s in range(2 * halo):
            LH[s] = LB[INTS[sends + s]]

    def spread(g, _):
        rows = pl.ds(pl.multiple_of(g * 8, 8), 8)
        keep = jnp.where(sub + g * 8 < INTS[sends + 2 * halo], 1.0, 0.0)
        for j in range(comp):
            XR[pl.ds(g * 64 + j, 8, stride=8), :] = keep * XIN[j, rows, :]
        for u in range(8):
            E0[g * 8 + u] = XB[g * 8 + u][:comp]
        return 0

    def start_state():
        term_copy.wait()
        lax.fori_loop(0, groups, spread, 0)
        for side, store in ((0, SLO), (1, SHI)):
            for s in range(halo):
                store[1, s] = XB[INTS[sends + side * halo + s]][:comp]
        start_side(0, 0, 1, lo, has_lo)
        start_side(1, 0, 1, hi, has_hi)

    def run_slab(K, SRC, LP, LPM, LB, LH, W, OUT, ends, began):
        for it in range(SWEEPS):
            level = STEPS - 1 - it // ITERS
            sweep = it % ITERS
            slot = it % SLOTS
            buf = it % 2

            def own(g, _):
                rows = pl.ds(pl.multiple_of(g * 8, 8), 8)
                xs = [XR[pl.ds(g * 64 + j, 8, stride=8), :] for j in range(comp)]
                cl, cr = CL[rows, :], CR[rows, :]
                for j in range(comp):
                    lp = LP[j, rows, :]
                    if sweep == 0:
                        v = lp * SRC[level, j, rows, :] + LPM[j, rows, :] * xs[j]
                        R[j, rows, :] = v
                    else:
                        v = R[j, rows, :]
                    for i in range(comp):
                        v = v + K[i, j, rows, :] * xs[i]
                    beside = cl * pltpu.roll(xs[j], 1, 1) + cr * pltpu.roll(xs[j], cells - 1, 1)
                    v = v + lp * beside
                    YR[pl.ds(g * 64 + j, 8, stride=8), :] = v
                return 0

            def spread_own(g, _):
                spread(g, 0)
                own(g, 0)
                return 0

            def arrive():
                for i in range(CHUNKS):
                    state_copy(i).wait_recv()
                    lax.fori_loop(i * groups // CHUNKS, (i + 1) * groups // CHUNKS, spread_own, 0)

            if it == 0 and not ends:
                arrive()
            elif it == 0:
                @pl.when(first)
                def _():
                    start_state()
                    lax.fori_loop(0, groups, own, 0)

                @pl.when(both(native, later))
                def _():
                    arrive()

                @pl.when(onpath)
                def _():
                    lax.fori_loop(0, groups, own, 0)
            else:
                lax.fori_loop(0, groups, own, 0)

            used = None
            if it >= 2:
                used = active
            elif ends:
                used = began if it == 0 else jnp.logical_or(began, first)
            if used is not None:
                for side, has in ((0, has_lo), (1, has_hi)):
                    @pl.when(both(used, has))
                    def _():
                        halo_copy(side, 0, buf, lo).wait_send()

            @pl.when(has_hi)
            def _():
                halo_copy(0, slot, buf, lo).wait_recv()

            @pl.when(has_lo)
            def _():
                halo_copy(1, slot, buf, hi).wait_recv()

            e, ahead = E[slot], E[(it + 1) % SLOTS]

            final = ends and it == SWEEPS - 1
            if final:
                to, after, go = (nlo, nhi), 0, more
            else:
                to, after, go = (lo, hi), (it + 1) % SLOTS, active
            for side, store, has in ((0, SLO, has_lo), (1, SHI, has_hi)):
                for s in range(halo):
                    at = side * halo + s
                    v = None
                    for k in range(nei):
                        t = FH[k, pl.ds(at, 1), :] * e[NH[at * nei + k]]
                        v = t if v is None else v + t
                    store[buf, s] = YB[INTS[sends + at]][:comp] + LH[at][:comp] * v
                start_side(side, after, buf, to[side], both(go, has))

            i = it % ITERS
            if it >= ITERS:
                go_home((0 if ends else 1), 1, i, last)
            elif ends:
                go_home(1, 0, i, last)

            def post(g, _):
                for u in range(8):
                    b = g * 8 + u
                    v = None
                    for k in range(nei):
                        t = F[k, pl.ds(b, 1), :] * e[INTS[k * nb + b]]
                        v = t if v is None else v + t
                    v = YB[b][:comp] + LB[b][:comp] * v
                    XB[b, pl.ds(0, comp), :] = v
                    ahead[b] = v
                return 0

            if sweep < ITERS - 1:
                lax.fori_loop(0, groups, post, 0)
                continue

            def post_level(g, _):
                post(g, 0)
                rows = pl.ds(pl.multiple_of(g * 8, 8), 8)
                acc = None
                for j in range(comp):
                    v = XR[pl.ds(g * 64 + j, 8, stride=8), :]
                    OUT[level, j, rows, :] = v
                    t = v * SH[j, rows, :]
                    acc = t if acc is None else acc + t
                ACC[rows, :] = ACC[rows, :] + W[level] * acc
                return 0

            if not final:
                lax.fori_loop(0, groups, post_level, 0)
            else:
                for i in range(CHUNKS):
                    lax.fori_loop(i * groups // CHUNKS, (i + 1) * groups // CHUNKS, post_level, 0)

                    @pl.when(more)
                    def _():
                        state_copy(i).start()

            if ends:
                for i in range(PIECES):
                    stay(level, i, False)

    def piece(i):
        cut = [j * groups // PIECES * 8 for j in range(PIECES + 1)]
        return pl.ds(cut[i], cut[i + 1] - cut[i])

    def home_copy(slab, level, i):
        out, sem, dev = (OUTA, oas, home_a) if slab else (OUTB, obs, home_b)
        return remote(out.at[level, :, piece(i)], adj_o.at[level, :, piece(i)],
                      sem.at[level, i], ors.at[level, i], dev)

    def here_copy(slab, level, i):
        out, sem = (OUTA, oas) if slab else (OUTB, obs)
        return pltpu.make_async_copy(out.at[level, :, piece(i)], adj_o.at[level, :, piece(i)],
                                     sem.at[level, i])

    def go_home(slab, level, i, cond, wait=False):
        def there():
            copy = home_copy(slab, level, i)
            copy.wait_send() if wait else copy.start()

        def here():
            copy = here_copy(slab, level, i)
            copy.wait() if wait else copy.start()

        if slab:
            pl.when(both(cond, self_a))(here)
            pl.when(both(cond, jnp.logical_not(self_a)))(there)
        else:
            pl.when(cond)(there)

    def stay(level, i, wait):
        @pl.when(native)
        def _():
            copy = here_copy(0, level, i)
            copy.wait() if wait else copy.start()

    def part_copy():
        return remote(PART, RED, pss, psr, nxt)

    def total_copy(t):
        return remote(PART, TOT, fss.at[t], fsr, (t, p))

    @pl.when(active)
    def _():
        zero = jnp.zeros((comp, cells), F32)
        for e in E:
            e[nb + 2 * halo] = zero

            @pl.when(jnp.logical_not(has_lo))
            def _():
                for s in range(halo):
                    e[nb + s] = zero

            @pl.when(jnp.logical_not(has_hi))
            def _():
                for s in range(halo):
                    e[nb + halo + s] = zero

        for g in range(groups):
            ACC[pl.ds(g * 8, 8), :] = jnp.zeros((8, cells), F32)

        @pl.when(native)
        def _():
            for copy in local:
                copy.wait()
            halo_tables()

        @pl.when(onpath)
        def _():
            for copy in coefficients(worker):
                copy.wait_recv()
            copy = pltpu.make_async_copy(IV, INTS, isem)
            copy.start()
            copy.wait()

            @pl.when(self_a)
            def _():
                for copy in self_operands:
                    copy.wait()

            @pl.when(jnp.logical_not(self_a))
            def _():
                for copy in slab_operands(KA, SRCA, WA, ra, worker):
                    copy.wait_recv()

            halo_tables()
            prepare_slab(KA, LPA, LPMA, LBA, LAR, LHA)
            for copy in slab_operands(KB, SRCB, WB, rb, worker):
                copy.wait_recv()

        prepare_slab(KB, LPB, LPMB, LBB, LBR, LHB)

        @pl.when(onpath)
        def _():
            run_slab(KA, SRCA, LPA, LPMA, LBA, LHA, WA, OUTA, False, None)

        run_slab(KB, SRCB, LPB, LPMB, LBB, LHB, WB, OUTB, True, onpath)

        early = both(onpath, jnp.logical_not(last))
        for i in range(PIECES):
            go_home(0, 0, i, onpath)

        PART[...] = jnp.sum(ACC[...].T, axis=0, keepdims=True)

        @pl.when(later)
        def _():
            part_copy().wait_recv()
            PART[...] = PART[...] + RED[...]

        @pl.when(more)
        def _():
            part_copy().start()

        @pl.when(last)
        def _():
            for t in range(n_tm):
                @pl.when(jnp.logical_not(same((t, p))))
                def _():
                    total_copy(t).start()

        for i in range(PIECES):
            go_home(1, 1, i, early)
            go_home(1, 0, i, early)
            go_home(0, 1, i, early)

    @pl.when(both(last, own_summer))
    def _():
        sens_o[...] = PART[...]

    @pl.when(jnp.logical_not(own_summer))
    def _():
        total_copy(0).wait_recv()
        sens_o[...] = TOT[...]

    @pl.when(last)
    def _():
        for t in range(n_tm):
            @pl.when(jnp.logical_not(same((t, p))))
            def _():
                total_copy(t).wait_send()

    @pl.when(more)
    def _():
        for i in range(CHUNKS):
            state_copy(i).wait_send()
        part_copy().wait_send()

    for side, has in ((0, has_lo), (1, has_hi)):
        @pl.when(both(active, has))
        def _():
            halo_copy(side, 0, (SWEEPS - 2) % 2, lo).wait_send()

        @pl.when(both(more, has))
        def _():
            halo_copy(side, 0, (SWEEPS - 1) % 2, lo).wait_send()

    for level in range(STEPS):
        for i in range(PIECES):
            go_home(1, level, i, onpath, True)
            go_home(0, level, i, onpath, True)
            stay(level, i, True)

    @pl.when(both(mover, odd, jnp.logical_not(own_worker)))
    def _():
        for copy in slab_operands(KA, SRCA, WA, ra, worker):
            copy.wait_send()

    @pl.when(both(mover, jnp.logical_not(odd)))
    def _():
        for copy in coefficients(worker):
            copy.wait_send()
        for copy in slab_operands(KB, SRCB, WB, rb, worker):
            copy.wait_send()

    @pl.when(both(mover, jnp.logical_not(own_worker)))
    def _():
        for level in range(STEPS):
            for i in range(PIECES):
                home_copy(0, level, i).wait_recv()


def per_device(source, terminal, jacobian, face_coef, cell_coef, neighbours, send_blocks,
               live_count, volume, shape_field, weights):
    nb, comp, cells = terminal.shape
    nei = face_coef.shape[1]
    halo = send_blocks.shape[2]
    anys = pl.BlockSpec(memory_space=pl.ANY)
    smem = pl.BlockSpec(memory_space=pltpu.SMEM)
    vmem = pltpu.VMEM
    dma = pltpu.SemaphoreType.DMA
    table = nb + 2 * halo + 1
    ints = jnp.concatenate(
        [
            neighbours.T.reshape(nei * nb),
            send_blocks.reshape(2 * halo),
            live_count,
            jnp.zeros(((8 - nei) * nb - 2 * halo - 1,), jnp.int32),
        ]
    )
    slab = vmem((comp, nb, cells), F32)
    plane = vmem((nb, cells), F32)
    rows8 = vmem((nb, 8, cells), F32)
    adj, sens = pl.pallas_call(
        kernel,
        out_shape=(
            jax.ShapeDtypeStruct((STEPS, comp, nb, cells), F32),
            jax.ShapeDtypeStruct((1, nb), F32),
        ),
        in_specs=[anys] * 8 + [smem],
        out_specs=(anys, pl.BlockSpec(memory_space=pltpu.VMEM)),
        scratch_shapes=[
            vmem((comp, comp, nb, cells), F32),
            vmem((comp, comp, nb, cells), F32),
            vmem((STEPS, comp, nb, cells), F32),
            vmem((STEPS, comp, nb, cells), F32),
            vmem((nei, nb, cells), F32),
            plane, plane, plane, plane,
            slab,
            slab, slab, slab, slab,
            rows8, rows8,
            slab, slab,
            rows8, rows8,
            vmem((table, comp, cells), F32),
            vmem((table, comp, cells), F32),
            vmem((table, comp, cells), F32),
            vmem((2, halo, comp, cells), F32),
            vmem((2, halo, comp, cells), F32),
            vmem((STEPS, comp, nb, cells), F32),
            vmem((STEPS, comp, nb, cells), F32),
            plane,
            vmem((1, nb), F32),
            vmem((1, nb), F32),
            vmem((1, nb), F32),
            vmem((STEPS, 1, cells), F32),
            vmem((STEPS, 1, cells), F32),
            vmem((STEPS, 1, cells), F32),
            vmem((8 * nb,), jnp.int32),
            pltpu.SMEM((8 * nb,), jnp.int32),
            vmem((nei, 2 * halo, cells), F32),
            vmem((2 * halo, 8, cells), F32),
            vmem((2 * halo, 8, cells), F32),
            pltpu.SMEM((2 * halo * nei,), jnp.int32),
            dma((3,)),
            dma((3,)),
            dma((3,)),
            dma((5,)),
            dma((5,)),
            dma(()),
            dma((CHUNKS,)),
            dma((SLOTS,)),
            dma((SLOTS,)),
            dma((2,)),
            dma((2,)),
            dma((STEPS, PIECES)),
            dma((STEPS, PIECES)),
            dma((STEPS, PIECES)),
            dma((CHUNKS,)),
            dma(()),
            dma(()),
            dma((lax.axis_size("tm"),)),
            dma(()),
        ],
        compiler_params=pltpu.CompilerParams(collective_id=0, has_side_effects=True),
        name="sweep",
    )(
        source.transpose(0, 2, 1, 3),
        terminal.transpose(1, 0, 2),
        jacobian.transpose(0, 2, 3, 1, 4),
        face_coef.transpose(1, 0, 2),
        cell_coef,
        ints,
        volume,
        shape_field.transpose(1, 0, 2),
        weights,
    )
    return adj.transpose(0, 2, 1, 3), sens.reshape(nb)


def solution(mesh):
    return jax.shard_map(
        per_device,
        mesh=mesh,
        in_specs=(
            P("tm", "space", None, None),
            P("space", None, None),
            P("tm", "space", None, None, None),
            P("space", None, None),
            P("space", None),
            P("space", None),
            P("space", None, None),
            P("space"),
            P("space", None),
            P("space", None, None),
            P("tm"),
        ),
        out_specs=(P("tm", "space", None, None), P("space")),
        check_vma=False,
    )
```

time: 1320 us -> 201 us (0.15); the launches traced: 1300 us -> 200 us
  starting transfers between devices: 477 us -> 0 us
  local copies, waits for them, and re-layouts: 369 us -> 3.9 us
  other arithmetic: 336 us -> 1.35 us
  Pallas kernels: 0 us -> 194 us
  waiting for transfers between devices: 106 us -> 0 us
    ppermute x103 -> x0, starting transfers between devices: 471 us -> none  [from_behind(): lax.ppermute(value, axis, [(source, source + steps) for source in range(f...]
    gather x144 -> x0, local copies, waits for them, and re-layouts: 312 us -> none  [the longest x48 174 us: operate(): gathered = extended[neighbours]]
    dot_general x96 -> x0, other arithmetic: 230 us -> none  [the longest x48 133 us: operate(): jnp.einsum('bnc,bnkc->bkc', face_coef, gathered, precision=highest)]
    pallas_call x0 -> x1, Pallas kernels: none -> 194 us  [per_device(): pl.pallas_call(kernel, out_shape=(jax.ShapeDtypeStruct((STEPS, comp, nb,...]
    ppermute x103 -> x0, waiting for transfers between devices: 102 us -> none  [from_behind(): lax.ppermute(value, axis, [(source, source + steps) for source in range(f...]
    mul x50 -> x0, other arithmetic: 50.2 us -> none  [the longest x48 49.9 us: level_step(): field = live * (field + precond * (rhs - operate(field, jac)))]
    while x748 -> x0, local copies, waits for them, and re-layouts: 38.7 us -> none
    concatenate x48 -> x1, other arithmetic: 31.5 us -> 1.35 us  [per_device(): jnp.concatenate([neighbours.T.reshape(nei * nb), send_blocks.reshape(2 *...]
  transfers between devices with their start and end apart: 104 -> 0, of which waited for: 33 -> 0; matrix products, arithmetic and copies ran while one was open for 12% -> 0% of each run, Pallas kernels for 0% -> 0%
where the time goes in v2:
time: 201 us; the launch traced here: 200 us
  Pallas kernels  194 us (97%)
  local copies, waits for them, and re-layouts  3.9 us (2%)
    pallas_call x1, Pallas kernels, per_device(): pl.pallas_call(kernel, out_shape=(jax.ShapeDtypeStruct((STEPS, comp, nb,...  194 us

profile of v2, /device:TPU:96, one launch (start us, length us, event | category | flops | bytes accessed | tf_op | source)
XLA Modules:
  0.0 200.3 jit_solution(4813057869076899247)
XLA Ops:
  1.3 0.8 reshape.14
  2.0 1.4 pad_add_fusion.ints_h
  3.4 193.8 %sweep.1 = (f32[2,5,128,128]{3,2,1,0:T(8,128)}, f32[1,128]{1,0:T(1,128)}) custom-call(f32[2,5,128,128]{3,2,1,0:T(8,128)} %bitcast.12, f32[5,128,128]{2,1,0:T(8,128)} %bitcast.14, f32[1,5,5,128,128]{4,3,2,1,0:T(8,128)} %bitcast.10, f32[6,128,128]{2,1,0:T(8,128)} %bitcast.13, f32[128,128]{1,0:T(8,128)} %cell_h.1, s32[1024]{0:T(1024)} %pad_add_fusion.ints_h, ...), custom_call_target="tpu_custom_call" | custom-call | tf_op jit(solution)/shard_map/sweep/pallas_call | solution.py:594
  197.2 2.0 copy.16
  199.2 1.2 copy.17
  (1 shorter events, 0.0 us)

commit v3 on v2

--- a/solution.py
+++ b/solution.py
@@ -26,13 +26,13 @@
     src_h, term_h, jac_h, face_h, cell_h, ints_h, vol_h, shape_h, w_s,
     adj_o, sens_o,
     KA, KB, SRCA, SRCB, F, CELL, CL, CR, VOL, SH, LPA, LPB, LPMA, LPMB, LBA, LBB,
-    R, XIN, XB, YB, E0, E1, E2, SLO, SHI, OUTA, OUTB, ACC, RED, PART, TOT,
-    WOUT, WA, WB, IV, INTS, FH, LHA, LHB, NH,
-    ra, rb, sa, rc, sc, isem, xr, elo, ehi, slo, shi, oas, obs, ors, hsem, psr, pss, fss, fsr,
+    R, XIN, XB, YB, E0, E1, E2, SV, SU, SSV, SSU, SF, OUTA, OUTB, ACC, RED, PART, TOT,
+    WOUT, WA, WB, IV, INTS, FH, LHA, LHB, NH, NHM, PIV, PINTS, PFH, PLHA, PLHB, PNH,
+    ra, rb, sa, rc, sc, vs, vr, vo, go_b, isem, xr, ef, ev, eu, sfs, svs, sus, pps, ppr, oas, obs, ors, hsem, psr, pss, fss, fsr,
 ):
     comp, nb, cells = XIN.shape
     nei = F.shape[0]
-    halo = SLO.shape[1]
+    halo = SF.shape[1]
     groups = nb // 8
     tm = lax.axis_index("tm")
     d = lax.axis_index("space")
@@ -75,13 +75,27 @@
 
     lo, hi = peer(p - 1), peer(p + 1)
     nxt = next_dev(p)
-    nlo, nhi = next_dev(p - 1), next_dev(p + 1)
+
+    up = p % 2 == 1
+    slow_q, fast_q = jnp.where(up, p + 1, p - 1), jnp.where(up, p - 1, p + 1)
+    has_slow = jnp.where(up, has_hi, has_lo)
+    slow, fast = peer(slow_q), peer(fast_q)
+    slow_next, fast_next = next_dev(slow_q), next_dev(fast_q)
+    slow_off, fast_off = jnp.where(up, halo, 0), jnp.where(up, 0, halo)
     home_a, home_b = (2 * x + 1, p), (2 * x, p)
     self_a = same(home_a)
     mover = jnp.logical_not(native)
     worker = path(x, d)
     own_worker = same(worker)
     odd = tm % 2 == 1
+
+    turned = both(mover, z % 2 == 1)
+    via_a, via_b = both(turned, y == 1, c == 0), both(turned, y == 2, c == 1)
+    via = jnp.logical_or(via_a, via_b)
+    relay_a, relay_b = both(turned, y == 0, c == 0), both(turned, y == 3, c == 0)
+    relay = pick(via_a, (2 * x, 4 * z), (2 * x + 1, 4 * z + 2))
+    relay_from = pick(relay_a, (2 * x + 1, 4 * z), (2 * x, 4 * z + 3))
+    relay_to = path(x, jnp.where(relay_a, 4 * z, 4 * z + 3))
     summer = path(0, d)
     own_summer = same(summer)
 
@@ -118,6 +132,12 @@
     edges.append((both(mover, jnp.logical_not(own_worker)), worker))
     edges.append((both(onpath, jnp.logical_not(self_a)), home_a))
     edges.append((onpath, home_b))
+    relays = jnp.logical_or(relay_a, relay_b)
+    edges.append((via, relay))
+    edges.append((relays, relay_from))
+    edges.append((relays, relay_to))
+    edges.append((both(onpath, z % 2 == 1, y == 3), (2 * x, 4 * z)))
+    edges.append((both(onpath, z % 2 == 1, y == 0), (2 * x + 1, 4 * z + 2)))
     for t in range(n_tm):
         edges.append((both(last, jnp.logical_not(same((t, p)))), (t, p)))
     edges.append((jnp.logical_not(own_summer), summer))
@@ -137,73 +157,61 @@
         def _():
             WB[level] = jnp.full((1, cells), w_s[level], F32)
 
-    pl.semaphore_wait(barrier, expect)
-
-    def coefficients(dev):
-        return [
-            remote(ints_h, IV, sc.at[4], rc.at[4], dev),
-            remote(face_h, F, sc.at[0], rc.at[0], dev),
-            remote(cell_h, CELL, sc.at[1], rc.at[1], dev),
-            remote(vol_h, VOL, sc.at[2], rc.at[2], dev),
-            remote(shape_h, SH, sc.at[3], rc.at[3], dev),
-        ]
-
-    def slab_operands(K, SRC, W, sems, dev):
-        return [
-            remote(jac_h.at[0], K, sa.at[0], sems.at[0], dev),
-            remote(src_h, SRC, sa.at[1], sems.at[1], dev),
-            remote(WOUT, W, sa.at[2], sems.at[2], dev),
-        ]
-
-    self_operands = [
-        pltpu.make_async_copy(jac_h.at[0], KA, ra.at[0]),
-        pltpu.make_async_copy(src_h, SRCA, ra.at[1]),
-    ]
-
-    @pl.when(both(mover, odd, jnp.logical_not(own_worker)))
-    def _():
-        for copy in slab_operands(KA, SRCA, WA, ra, worker):
-            copy.start()
-
-    @pl.when(both(mover, odd, own_worker))
-    def _():
-        for copy in self_operands:
-            copy.start()
-        WA[...] = WOUT[...]
-
-    @pl.when(both(mover, jnp.logical_not(odd)))
-    def _():
-        for copy in coefficients(worker):
-            copy.start()
-        for copy in slab_operands(KB, SRCB, WB, rb, worker):
-            copy.start()
-
     E = (E0, E1, E2)
     XR, YR, LAR, LBR = (ref.reshape(ref.shape[0] * 8, cells) for ref in (XB, YB, LBA, LBB))
     lane = lax.broadcasted_iota(jnp.int32, (8, cells), 1)
     sub = lax.broadcasted_iota(jnp.int32, (8, cells), 0)
     sends = nei * nb
 
-    def halo_copy(side, slot, buf, dev):
-        if side == 0:
-            return remote(SLO.at[buf], E[slot].at[pl.ds(nb + halo, halo)], slo.at[buf], ehi.at[slot], dev)
-        return remote(SHI.at[buf], E[slot].at[pl.ds(nb, halo)], shi.at[buf], elo.at[slot], dev)
-
-    def start_side(side, slot, buf, dev, cond):
-        @pl.when(cond)
-        def _():
-            halo_copy(side, slot, buf, dev).start()
+    def fast_copy(slot, buf, dev):
+        return remote(SF.at[buf], E[slot].at[pl.ds(nb + slow_off, halo)], sfs.at[buf], ef.at[slot], dev)
+
+    def whole_copy(m, dev):
+        return remote(SSV.at[pl.ds(0, halo)], SV.at[m], svs, ev.at[m], dev)
+
+    def part_of_copy(m, dev):
+        return remote(SSU, SU.at[m], sus, eu.at[m], dev)
 
     def state_copy(i):
         rows = pl.ds(i * (nb // CHUNKS), nb // CHUNKS)
         return remote(OUTB.at[0, :, rows], XIN.at[:, rows], hsem.at[i], xr.at[i], nxt)
 
+    def sent(at):
+        side, s = at // halo, at % halo
+        return INTS[sends + (fast_off if side else slow_off) + s]
+
     def halo_tables():
         for s in range(2 * halo):
-            b = INTS[sends + s]
+            b = sent(s)
             for k in range(nei):
-                NH[s * nei + k] = INTS[k * nb + b]
+                n = INTS[k * nb + b]
+                NH[s * nei + k] = n
+                if s < halo:
+                    r = n - (nb + slow_off)
+                    NHM[s * nei + k] = jnp.where((r >= 0) & (r < halo), nb + 2 * halo, n)
                 FH[k, pl.ds(s, 1), :] = F[k, b][None, :]
+
+    def peer_face():
+        return remote(FH.at[:, pl.ds(0, halo)], PFH, pps.at[0], ppr.at[0], slow)
+
+    def peer_copy_b():
+        return remote(LHB.at[pl.ds(0, halo)], PLHB, pps.at[1], ppr.at[1], slow)
+
+    def peer_copy_a():
+        return remote(LHA.at[pl.ds(0, halo)], PLHA, pps.at[2], ppr.at[2], slow)
+
+    def peer_ints(src):
+        return remote(src, PIV, pps.at[3], ppr.at[3], slow)
+
+    def peer_tables():
+        copy = pltpu.make_async_copy(PIV, PINTS, isem)
+        copy.start()
+        copy.wait()
+        for s in range(halo):
+            b = PINTS[sends + fast_off + s]
+            for k in range(nei):
+                r = PINTS[k * nb + b] - (nb + fast_off)
+                PNH[s * nei + k] = jnp.where((r >= 0) & (r < halo), r, halo)
 
     def prepare_slab(K, LP, LPM, LB, LPR, LH):
         lc = INTS[sends + 2 * halo]
@@ -233,7 +241,98 @@
 
         lax.fori_loop(0, groups, prepare, 0)
         for s in range(2 * halo):
-            LH[s] = LB[INTS[sends + s]]
+            LH[s] = LB[sent(s)]
+
+    @pl.when(native)
+    def _():
+        for copy in local:
+            copy.wait()
+        halo_tables()
+        prepare_slab(KB, LPB, LPMB, LBB, LBR, LHB)
+
+    pl.semaphore_wait(barrier, expect)
+
+    @pl.when(both(native, has_slow))
+    def _():
+        remote(ints_h, PIV, pps.at[3], ppr.at[3], slow).start()
+
+    def coefficients(dev):
+        return [
+            remote(ints_h, IV, sc.at[4], rc.at[4], dev),
+            remote(face_h, F, sc.at[0], rc.at[0], dev),
+            remote(cell_h, CELL, sc.at[1], rc.at[1], dev),
+            remote(vol_h, VOL, sc.at[2], rc.at[2], dev),
+            remote(shape_h, SH, sc.at[3], rc.at[3], dev),
+        ]
+
+    def slab_operands(K, SRC, W, sems, dev):
+        return [
+            remote(jac_h.at[0], K, sa.at[0], sems.at[0], dev),
+            remote(src_h, SRC, sa.at[1], sems.at[1], dev),
+            remote(WOUT, W, sa.at[2], sems.at[2], dev),
+        ]
+
+    def operand_pieces(source):
+        if source:
+            refs = [(jac_h.at[0, i], KA.at[i]) for i in range(comp)]
+            refs += [(src_h.at[i], SRCA.at[i]) for i in range(STEPS)]
+            return [remote(a, b, vs.at[i], vr.at[i], relay) for i, (a, b) in enumerate(refs)]
+        out = []
+        for K, SRC, sems in ((KA, SRCA, ra), (KB, SRCB, rb)):
+            refs = [(KA.at[i], K.at[i], sems.at[0]) for i in range(comp)]
+            refs += [(SRCA.at[i], SRC.at[i], sems.at[1]) for i in range(STEPS)]
+            out.append([remote(a, b, vo.at[i], sem, relay_to) for i, (a, b, sem) in enumerate(refs)])
+        return out
+
+    def send_operands(K, SRC, W, sems, wait):
+        copies = slab_operands(K, SRC, W, sems, worker)
+
+        @pl.when(jnp.logical_not(via))
+        def _():
+            for copy in copies[:2]:
+                copy.wait_send() if wait else copy.start()
+
+        @pl.when(via)
+        def _():
+            for copy in operand_pieces(True):
+                copy.wait_send() if wait else copy.start()
+
+        copies[2].wait_send() if wait else copies[2].start()
+
+    self_operands = [
+        pltpu.make_async_copy(jac_h.at[0], KA, ra.at[0]),
+        pltpu.make_async_copy(src_h, SRCA, ra.at[1]),
+    ]
+
+    @pl.when(both(mover, odd, jnp.logical_not(own_worker)))
+    def _():
+        send_operands(KA, SRCA, WA, ra, False)
+
+    @pl.when(both(mover, odd, own_worker))
+    def _():
+        for copy in self_operands:
+            copy.start()
+        WA[...] = WOUT[...]
+
+    @pl.when(both(mover, jnp.logical_not(odd)))
+    def _():
+        for copy in coefficients(worker):
+            copy.start()
+
+    @pl.when(relays)
+    def _():
+        arriving = operand_pieces(True)
+        onward_a, onward_b = operand_pieces(False)
+        for i in range(comp + STEPS):
+            arriving[i].wait_recv()
+            pl.when(relay_a)(onward_a[i].start)
+            pl.when(relay_b)(onward_b[i].start)
+
+    def send_even():
+        pl.semaphore_wait(go_b, 1)
+        send_operands(KB, SRCB, WB, rb, False)
+
+    pl.when(both(mover, jnp.logical_not(odd), c == 0))(send_even)
 
     def spread(g, _):
         rows = pl.ds(pl.multiple_of(g * 8, 8), 8)
@@ -247,13 +346,17 @@
     def start_state():
         term_copy.wait()
         lax.fori_loop(0, groups, spread, 0)
-        for side, store in ((0, SLO), (1, SHI)):
-            for s in range(halo):
-                store[1, s] = XB[INTS[sends + side * halo + s]][:comp]
-        start_side(0, 0, 1, lo, has_lo)
-        start_side(1, 0, 1, hi, has_hi)
-
-    def run_slab(K, SRC, LP, LPM, LB, LH, W, OUT, ends, began):
+        for s in range(halo):
+            SSV[s] = XB[sent(s)][:comp]
+            SF[1, s] = XB[sent(halo + s)][:comp]
+
+        @pl.when(has_slow)
+        def _():
+            whole_copy(0, slow).start()
+
+        fast_copy(0, 1, fast).start()
+
+    def run_slab(K, SRC, LP, LPM, LB, LH, PLH, W, OUT, ends, began):
         for it in range(SWEEPS):
             level = STEPS - 1 - it // ITERS
             sweep = it % ITERS
@@ -287,6 +390,8 @@
                 for i in range(CHUNKS):
                     state_copy(i).wait_recv()
                     lax.fori_loop(i * groups // CHUNKS, (i + 1) * groups // CHUNKS, spread_own, 0)
+                for s in range(halo):
+                    SSV[s] = XB[sent(s)][:comp]
 
             if it == 0 and not ends:
                 arrive()
@@ -312,35 +417,73 @@
             elif ends:
                 used = began if it == 0 else jnp.logical_or(began, first)
             if used is not None:
-                for side, has in ((0, has_lo), (1, has_hi)):
-                    @pl.when(both(used, has))
+                @pl.when(used)
+                def _():
+                    fast_copy(0, buf, fast).wait_send()
+
+                @pl.when(both(used, has_slow))
+                def _():
+                    (whole_copy(0, slow) if it % 2 else part_of_copy(0, slow)).wait_send()
+
+            e, ahead = E[slot], E[(it + 1) % SLOTS]
+            pair = it // 2
+
+            def entry(at, table):
+                v = None
+                for k in range(nei):
+                    t = FH[k, pl.ds(at, 1), :] * e[table[at * nei + k]]
+                    v = t if v is None else v + t
+                return YB[sent(at)][:comp] + LH[at][:comp] * v
+
+            final = ends and it == SWEEPS - 1
+            go = more if final else active
+            if it % 2 == 0:
+                fast_copy(slot, buf, fast).wait_recv()
+                for s in range(halo):
+                    SSU[s] = entry(s, NHM)
+
+                @pl.when(has_slow)
+                def _():
+                    part_of_copy(pair, slow).start()
+                    whole_copy(pair, slow).wait_recv()
+                    for s in range(halo):
+                        e[nb + slow_off + s] = SV[pair, s]
+            else:
+                if it == 1 and ends:
+                    @pl.when(has_slow)
                     def _():
-                        halo_copy(side, 0, buf, lo).wait_send()
-
-            @pl.when(has_hi)
+                        peer_copy_b().wait_recv()
+
+                    @pl.when(both(native, has_slow))
+                    def _():
+                        peer_face().wait_recv()
+                        peer_ints(ints_h).wait_recv()
+                        peer_tables()
+
+                @pl.when(has_slow)
+                def _():
+                    part_of_copy(pair, slow).wait_recv()
+                    for s in range(halo):
+                        v = None
+                        for k in range(nei):
+                            t = PFH[k, pl.ds(s, 1), :] * SSV[PNH[s * nei + k]]
+                            v = t if v is None else v + t
+                        e[nb + slow_off + s] = SU[pair, s] + PLH[s][:comp] * v
+
+                fast_copy(slot, buf, fast).wait_recv()
+                for s in range(halo):
+                    SSV[s] = entry(s, NH)
+
+                @pl.when(both(go, has_slow))
+                def _():
+                    whole_copy((pair + 1) % 3, slow_next if final else slow).start()
+
+            for s in range(halo):
+                SF[buf, s] = entry(halo + s, NH)
+
+            @pl.when(go)
             def _():
-                halo_copy(0, slot, buf, lo).wait_recv()
-
-            @pl.when(has_lo)
-            def _():
-                halo_copy(1, slot, buf, hi).wait_recv()
-
-            e, ahead = E[slot], E[(it + 1) % SLOTS]
-
-            final = ends and it == SWEEPS - 1
-            if final:
-                to, after, go = (nlo, nhi), 0, more
-            else:
-                to, after, go = (lo, hi), (it + 1) % SLOTS, active
-            for side, store, has in ((0, SLO, has_lo), (1, SHI, has_hi)):
-                for s in range(halo):
-                    at = side * halo + s
-                    v = None
-                    for k in range(nei):
-                        t = FH[k, pl.ds(at, 1), :] * e[NH[at * nei + k]]
-                        v = t if v is None else v + t
-                    store[buf, s] = YB[INTS[sends + at]][:comp] + LH[at][:comp] * v
-                start_side(side, after, buf, to[side], both(go, has))
+                fast_copy((it + 1) % SLOTS, buf, fast_next if final else fast).start()
 
             i = it % ITERS
             if it >= ITERS:
@@ -437,24 +580,14 @@
         for e in E:
             e[nb + 2 * halo] = zero
 
-            @pl.when(jnp.logical_not(has_lo))
+            @pl.when(jnp.logical_not(has_slow))
             def _():
                 for s in range(halo):
-                    e[nb + s] = zero
-
-            @pl.when(jnp.logical_not(has_hi))
-            def _():
-                for s in range(halo):
-                    e[nb + halo + s] = zero
-
+                    e[nb + slow_off + s] = zero
+
+        SSV[halo] = zero
         for g in range(groups):
             ACC[pl.ds(g * 8, 8), :] = jnp.zeros((8, cells), F32)
-
-        @pl.when(native)
-        def _():
-            for copy in local:
-                copy.wait()
-            halo_tables()
 
         @pl.when(onpath)
         def _():
@@ -464,6 +597,10 @@
             copy.start()
             copy.wait()
 
+            @pl.when(has_slow)
+            def _():
+                peer_ints(IV).start()
+
             @pl.when(self_a)
             def _():
                 for copy in self_operands:
@@ -474,18 +611,42 @@
                 for copy in slab_operands(KA, SRCA, WA, ra, worker):
                     copy.wait_recv()
 
+            pl.semaphore_signal(go_b, 1, device_id=home_b, device_id_type=MESH)
+            pl.when(jnp.logical_not(odd))(send_even)
             halo_tables()
             prepare_slab(KA, LPA, LPMA, LBA, LAR, LHA)
+
+            @pl.when(has_slow)
+            def _():
+                peer_face().start()
+                peer_copy_a().start()
+                for copy in (peer_ints(IV), peer_face(), peer_copy_a()):
+                    copy.wait_recv()
+                peer_tables()
+
+        def take_b():
             for copy in slab_operands(KB, SRCB, WB, rb, worker):
                 copy.wait_recv()
-
-        prepare_slab(KB, LPB, LPMB, LBB, LBR, LHB)
+            prepare_slab(KB, LPB, LPMB, LBB, LBR, LHB)
+
+            @pl.when(has_slow)
+            def _():
+                peer_copy_b().start()
+
+        rushed = x == n_planes - 2
+        pl.when(both(onpath, jnp.logical_not(rushed)))(take_b)
+
+        @pl.when(both(native, has_slow))
+        def _():
+            peer_face().start()
+            peer_copy_b().start()
 
         @pl.when(onpath)
         def _():
-            run_slab(KA, SRCA, LPA, LPMA, LBA, LHA, WA, OUTA, False, None)
-
-        run_slab(KB, SRCB, LPB, LPMB, LBB, LHB, WB, OUTB, True, onpath)
+            run_slab(KA, SRCA, LPA, LPMA, LBA, LHA, PLHA, WA, OUTA, False, None)
+            pl.when(rushed)(take_b)
+
+        run_slab(KB, SRCB, LPB, LPMB, LBB, LHB, PLHB, WB, OUTB, True, onpath)
 
         early = both(onpath, jnp.logical_not(last))
         for i in range(PIECES):
@@ -536,14 +697,28 @@
             state_copy(i).wait_send()
         part_copy().wait_send()
 
-    for side, has in ((0, has_lo), (1, has_hi)):
-        @pl.when(both(active, has))
-        def _():
-            halo_copy(side, 0, (SWEEPS - 2) % 2, lo).wait_send()
-
-        @pl.when(both(more, has))
-        def _():
-            halo_copy(side, 0, (SWEEPS - 1) % 2, lo).wait_send()
+    @pl.when(active)
+    def _():
+        fast_copy(0, (SWEEPS - 2) % 2, fast).wait_send()
+
+    @pl.when(more)
+    def _():
+        fast_copy(0, (SWEEPS - 1) % 2, fast).wait_send()
+
+    @pl.when(both(active, has_slow))
+    def _():
+        part_of_copy(0, slow).wait_send()
+        peer_ints(IV).wait_send()
+        peer_face().wait_send()
+        peer_copy_b().wait_send()
+
+    @pl.when(both(onpath, has_slow))
+    def _():
+        peer_copy_a().wait_send()
+
+    @pl.when(both(more, has_slow))
+    def _():
+        whole_copy(0, slow).wait_send()
 
     for level in range(STEPS):
         for i in range(PIECES):
@@ -553,15 +728,20 @@
 
     @pl.when(both(mover, odd, jnp.logical_not(own_worker)))
     def _():
-        for copy in slab_operands(KA, SRCA, WA, ra, worker):
-            copy.wait_send()
+        send_operands(KA, SRCA, WA, ra, True)
 
     @pl.when(both(mover, jnp.logical_not(odd)))
     def _():
         for copy in coefficients(worker):
             copy.wait_send()
-        for copy in slab_operands(KB, SRCB, WB, rb, worker):
-            copy.wait_send()
+        send_operands(KB, SRCB, WB, rb, True)
+
+    @pl.when(relays)
+    def _():
+        onward_a, onward_b = operand_pieces(False)
+        for i in range(comp + STEPS):
+            pl.when(relay_a)(onward_a[i].wait_send)
+            pl.when(relay_b)(onward_b[i].wait_send)
 
     @pl.when(both(mover, jnp.logical_not(own_worker)))
     def _():
@@ -614,7 +794,10 @@
             vmem((table, comp, cells), F32),
             vmem((table, comp, cells), F32),
             vmem((table, comp, cells), F32),
-            vmem((2, halo, comp, cells), F32),
+            vmem((3, halo, comp, cells), F32),
+            vmem((3, halo, comp, cells), F32),
+            vmem((halo + 1, comp, cells), F32),
+            vmem((halo, comp, cells), F32),
             vmem((2, halo, comp, cells), F32),
             vmem((STEPS, comp, nb, cells), F32),
             vmem((STEPS, comp, nb, cells), F32),
@@ -631,17 +814,32 @@
             vmem((2 * halo, 8, cells), F32),
             vmem((2 * halo, 8, cells), F32),
             pltpu.SMEM((2 * halo * nei,), jnp.int32),
+            pltpu.SMEM((halo * nei,), jnp.int32),
+            vmem((8 * nb,), jnp.int32),
+            pltpu.SMEM((8 * nb,), jnp.int32),
+            vmem((nei, halo, cells), F32),
+            vmem((halo, 8, cells), F32),
+            vmem((halo, 8, cells), F32),
+            pltpu.SMEM((halo * nei,), jnp.int32),
             dma((3,)),
             dma((3,)),
             dma((3,)),
             dma((5,)),
             dma((5,)),
+            dma((comp + STEPS,)),
+            dma((comp + STEPS,)),
+            dma((comp + STEPS,)),
+            pltpu.SemaphoreType.REGULAR,
             dma(()),
             dma((CHUNKS,)),
             dma((SLOTS,)),
-            dma((SLOTS,)),
+            dma((3,)),
+            dma((3,)),
             dma((2,)),
-            dma((2,)),
+            dma(()),
+            dma(()),
+            dma((4,)),
+            dma((4,)),
             dma((STEPS, PIECES)),
             dma((STEPS, PIECES)),
             dma((STEPS, PIECES)),

time: 201 us -> 198 us (0.985)
  Pallas kernels: 194 us -> 191 us
    pallas_call x1, Pallas kernels: 194 us -> 191 us  [per_device(): pl.pallas_call(kernel, out_shape=(jax.ShapeDtypeStruct((STEPS, comp, nb,...]
where the time goes in v3:
time: 198 us
  Pallas kernels  191 us (96%)
  local copies, waits for them, and re-layouts  3.9 us (2%)
    pallas_call x1, Pallas kernels, per_device(): pl.pallas_call(kernel, out_shape=(jax.ShapeDtypeStruct((STEPS, comp, nb,...  191 us

profile of v3, /device:TPU:96, one launch (start us, length us, event | category | flops | bytes accessed | tf_op | source)
XLA Modules:
  0.0 197.6 jit_solution(18231779805678617938)
XLA Ops:
  1.3 0.8 reshape.14
  2.0 1.4 pad_add_fusion.ints_h
  3.4 191.1 %sweep.1 = (f32[2,5,128,128]{3,2,1,0:T(8,128)}, f32[1,128]{1,0:T(1,128)}) custom-call(f32[2,5,128,128]{3,2,1,0:T(8,128)} %bitcast.12, f32[5,128,128]{2,1,0:T(8,128)} %bitcast.14, f32[1,5,5,128,128]{4,3,2,1,0:T(8,128)} %bitcast.10, f32[6,128,128]{2,1,0:T(8,128)} %bitcast.13, f32[128,128]{1,0:T(8,128)} %cell_h.1, s32[1024]{0:T(1024)} %pad_add_fusion.ints_h, ...), custom_call_target="tpu_custom_call" | custom-call | tf_op jit(solution)/shard_map/sweep/pallas_call | solution.py:774
  194.5 2.0 copy.16
  196.4 1.2 copy.17
  (1 shorter events, 0.0 us)

commit v4 on v3

--- a/solution.py
+++ b/solution.py
@@ -11,7 +11,7 @@
 STEPS = 2
 SWEEPS = ITERS * STEPS
 SLOTS = 3
-CHUNKS = 4
+CHUNKS = 8
 PIECES = 3
 INVERSE_STEP = 6.0
 MESH = pl.DeviceIdType.MESH
@@ -437,6 +437,9 @@
 
             final = ends and it == SWEEPS - 1
             go = more if final else active
+
+            def taken(f):
+                pl.when(more)(f) if final else f()
             if it % 2 == 0:
                 fast_copy(slot, buf, fast).wait_recv()
                 for s in range(halo):
@@ -471,15 +474,21 @@
                         e[nb + slow_off + s] = SU[pair, s] + PLH[s][:comp] * v
 
                 fast_copy(slot, buf, fast).wait_recv()
-                for s in range(halo):
-                    SSV[s] = entry(s, NH)
+                def whole():
+                    for s in range(halo):
+                        SSV[s] = entry(s, NH)
+
+                taken(whole)
 
                 @pl.when(both(go, has_slow))
                 def _():
                     whole_copy((pair + 1) % 3, slow_next if final else slow).start()
 
-            for s in range(halo):
-                SF[buf, s] = entry(halo + s, NH)
+            def quick():
+                for s in range(halo):
+                    SF[buf, s] = entry(halo + s, NH)
+
+            taken(quick)
 
             @pl.when(go)
             def _():
@@ -529,6 +538,10 @@
                     def _():
                         state_copy(i).start()
 
+                    for j in range(PIECES):
+                        if i * groups // CHUNKS < (j + 1) * groups // PIECES <= (i + 1) * groups // CHUNKS:
+                            go_home(0, 0, j, last)
+
             if ends:
                 for i in range(PIECES):
                     stay(level, i, False)
@@ -650,7 +663,7 @@
 
         early = both(onpath, jnp.logical_not(last))
         for i in range(PIECES):
-            go_home(0, 0, i, onpath)
+            go_home(0, 0, i, early)
 
         PART[...] = jnp.sum(ACC[...].T, axis=0, keepdims=True)
 
@@ -763,7 +776,8 @@
     ints = jnp.concatenate(
         [
             neighbours.T.reshape(nei * nb),
-            send_blocks.reshape(2 * halo),
+            send_blocks[0, 0],
+            send_blocks[0, 1],
             live_count,
             jnp.zeros(((8 - nei) * nb - 2 * halo - 1,), jnp.int32),
         ]

time: 198 us -> 197 us (level)
  no operation moved by 1% of the time
where the time goes in v4:
time: 197 us
  Pallas kernels  190 us (96%)
  local copies, waits for them, and re-layouts  5.22 us (3%)
    pallas_call x1, Pallas kernels, per_device(): pl.pallas_call(kernel, out_shape=(jax.ShapeDtypeStruct((STEPS, comp, nb,...  190 us

profile of v4, /device:TPU:96, one launch (start us, length us, event | category | flops | bytes accessed | tf_op | source)
XLA Modules:
  0.0 196.5 jit_solution(11284489764081538375)
XLA Ops:
  1.3 0.8 slice_bitcast_fusion
  2.0 1.3 concatenate.3.ints_h
  3.4 190.0 %sweep.1 = (f32[2,5,128,128]{3,2,1,0:T(8,128)}, f32[1,128]{1,0:T(1,128)}) custom-call(f32[2,5,128,128]{3,2,1,0:T(8,128)} %bitcast.16, f32[5,128,128]{2,1,0:T(8,128)} %bitcast.18, f32[1,5,5,128,128]{4,3,2,1,0:T(8,128)} %bitcast.14, f32[6,128,128]{2,1,0:T(8,128)} %bitcast.17, f32[128,128]{1,0:T(8,128)} %cell_h.1, s32[1024]{0:T(1024)} %concatenate.3.ints_h, ...), custom_call_target="tpu_custom_call" | custom-call | tf_op jit(solution)/shard_map/sweep/pallas_call | solution.py:788
  193.4 2.0 %copy.16 = f32[2,128,5,128]{3,1,2,0:T(8,128)} copy(f32[2,128,5,128]{3,1,2,0:T(8,128)} %bitcast.15) | data formatting | bytes 1310720
  195.4 1.1 copy.17
  (1 shorter events, 0.0 us)
